TPU v7x, 128 devices: a whole 4x4x4 slice. The times are simulated.
128 devices in a mesh: swath: 32 (over x, y, core), chan: 4 (over z).
Axes of the slice: x: 4, y: 4, z: 4, core: 2. Of those that a mesh axis runs over, the one named last changes fastest.
Arguments:
- innovations: float32 [2097152], P(('swath', 'chan')), may hold values from -6 to 6
- obs_precision: float32 [2097152], P(('swath', 'chan')), may hold values from 0.25 to 4
- jacobian: bfloat16 [2097152, 128], P(('swath', 'chan')), may hold values from -0.5 to 0.5
- predictors: float32 [8, 2097152], P(None, ('swath', 'chan')), may hold values from -5 to 5
- obs_column: int32 [2097152], P(('swath', 'chan')), may hold values from 0 to 2047, as said below
- obs_channel: int32 [2097152], P(('swath', 'chan')), may hold values from 0 to 5119
- obs_count: int32 [32, 4], P('swath', 'chan'), may hold values from 5461 to 16384, as said below
- smoothing: float32 [128], replicated, may hold values from 0.02 to 0.12
- bias_precision: float32 [8, 5120], P(None, 'chan'), may hold values from 1 to 100
Outputs:
- control_state: float32 [1024, 256, 128], P('swath', 'chan')
- bias_increment: float32 [8, 5120], P(None, 'chan')
- residual_norms: float32 [3], replicated
Inputs may be any that keep to these rules, and one draw needn't show every extreme that they name: `obs_column`: Row-major index latitude row * 64 + longitude column within the tile of the device that holds the slot; all slots of an aligned block of 128 slots lie in one latitude row. `obs_channel`: channel c belongs to block c // 256, whose coefficients are owned by chan index c // 1280. `obs_count`: slots below the count hold live observations, the rest are ignored; some device is full in every draw.
All inputs are finite; a program needn't handle non-finite values.
Results may differ from a plain program's by a relative error of at most 0.0003.
Values sent between devices are 32-bit elements; how exact they have to be, the bound alone decides.
A program may use at most 128 MiB of HBM per device.

v0:
```python
import jax
import jax.numpy as jnp
from jax import lax
from jax.experimental import pallas as pl
from jax.experimental.pallas import tpu as pltpu
from jax.sharding import Mesh
from jax.sharding import PartitionSpec as P

LEV = 128
NPRED = 8
LINES = 128
LAT = 32
LON = 64
TILES = 40
AX = ("swath_0", "swath_1", "swath_2", "chan")
SWATH = AX[:3]
MESH = pl.DeviceIdType.MESH
NT = (((1,), (1,)), ((), ()))
bf16, f32, i32 = jnp.bfloat16, jnp.float32, jnp.int32
KL = 8
UN = 8


def split(t):
    hi = t.astype(bf16)
    return hi, (t - hi.astype(f32)).astype(bf16)


def bc(row, n):
    return jnp.broadcast_to(row, (n, 128))


def lanes(b):
    return pl.ds(pl.multiple_of(b * 128, 128), 128)


def sum8(x):
    return jnp.sum(x, axis=0, keepdims=True)


def lookup(tab, ch_ref, pred_ref, out_ref):
    def step(i, _):
        for u in range(UN):
            b = i * UN + u
            ch = bc(ch_ref[pl.ds(b, 1), :], 8)
            lo, hi = ch & 127, ch >> 7
            acc = jnp.zeros((8, 128), f32)
            for h in range(TILES):
                g = jnp.take_along_axis(tab[h], lo, axis=1, mode="promise_in_bounds")
                acc = jnp.where(hi == h, g, acc)
            out_ref[pl.ds(b, 1), :] = sum8(acc * pred_ref[:, lanes(b)])
        return 0

    lax.fori_loop(0, LINES // UN, step, 0)


def forward(u2, jac, sm_i, col_ref, out_ref):
    iota = lax.broadcasted_iota(i32, (LON, 128), 0)

    def step(i, _):
        for u in range(UN):
            b = i * UN + u
            both = lax.dot_general(u2[sm_i[4, b]], jac[b], NT, preferred_element_type=f32)
            s = both[:LON] + both[LON:]
            m = iota == bc(col_ref[pl.ds(b, 1), :], LON)
            out_ref[pl.ds(b, 1), :] = sum8(jnp.where(m, s, 0.0))
        return 0

    lax.fori_loop(0, LINES // UN, step, 0)


def adjoint(y_ref, jac, sm_i, col_ref, seg):
    iota = lax.broadcasted_iota(i32, (LON, 128), 0)

    def step(i, acc):
        for u in range(UN):
            k = i * UN + u
            b = sm_i[0, k]
            y = y_ref[pl.ds(b, 1), :]
            hi = y.astype(bf16).astype(f32)
            lo = y - hi
            m = iota == bc(col_ref[pl.ds(b, 1), :], LON)
            parts = [jnp.where(m, bc(t, LON), 0.0) for t in (hi, lo)]
            a = jnp.concatenate(parts, axis=0).astype(bf16)
            both = jnp.dot(a, jac[b], preferred_element_type=f32)
            same = sm_i[1, k] == sm_i[1, jnp.maximum(k - 1, 0)]
            acc = jnp.where(same, acc, 0.0) + (both[:LON] + both[LON:])
            seg[k] = acc
        return acc

    lax.fori_loop(0, LINES // UN, step, jnp.zeros((LON, 128), f32))


def make_hot(ch_ref, oh):
    iota = lax.broadcasted_iota(i32, (256, 128), 0)

    def step(b, _):
        ch = ch_ref[pl.ds(b, 1), :] & 255
        oh[:, lanes(b)] = jnp.where(iota == bc(ch, 256), 1.0, 0.0).astype(bf16)
        return 0

    lax.fori_loop(0, LINES, step, 0)


def bias_adjoint(terms, ch_ref, oh, lhs, acc):
    rows, k = 320 * len(terms), KL * 128

    def step(c, _):
        for l in range(KL):
            b = c * KL + l
            hb = bc((ch_ref[pl.ds(b, 1), :] >> 8).astype(f32), 16).astype(bf16)
            for j, f in enumerate(terms):
                st = jnp.concatenate(split(f(b)), axis=0)
                for h in range(20):
                    at = (j * 20 + h) * 16
                    lhs[at : at + 16, l * 128 : (l + 1) * 128] = jnp.where(
                        hb == jnp.asarray(h, bf16), st, jnp.zeros((), bf16)
                    )
        part = lax.dot_general(
            lhs[:rows], oh[:, pl.ds(pl.multiple_of(c * k, k), k)], NT, preferred_element_type=f32
        )
        acc[:rows] += part
        return 0

    acc[:rows] = jnp.zeros((rows, 256), f32)
    lax.fori_loop(0, LINES // KL, step, 0)


def acc_tile(acc, j, t):
    at, ls = (j * 20 + t // 2) * 16, slice((t % 2) * 128, (t % 2) * 128 + 128)
    return acc[at : at + 8, ls] + acc[at + 8 : at + 16, ls]


def wait_all(ref, sem):
    pltpu.make_async_copy(ref, ref, sem).wait()


def kernel(
    innov, prec, jac_hbm, pred, col, chan, count, smooth, biasp,
    out_x, out_b, out_n,
    jac, oh, lhs, acc, w, y, hs, pc, u2, seg, gp, r0, r1, q0, xs, est, hcol, cn,
    rs0_send, rs0_recv, rs_send, rs_recv, zt, sca, scb, ob, iv, cl, sm_i,
    s_load, s_halo_s, s_halo_r, s_rs_s, s_rs_r, s_ag_s, s_ag_r, s_sc_s, s_sc_r,
):
    x, yy, c, z = (lax.axis_index(a) for a in AX)
    s = (x * 4 + yy) * 2 + c
    owner = (lax.rem(s, 3) == 0) & (s < 30)
    mine = z * 10 + lax.div(s, 3)
    me = s * 4 + z

    def coords(sw):
        return lax.div(sw, 8), lax.rem(lax.div(sw, 2), 4), lax.rem(sw, 2)

    load_j = pltpu.make_async_copy(jac_hbm, jac, s_load.at[0])
    load_j.start()
    for ph in range(3):
        for r in (0, 1, 34, 35):
            gp[ph, r] = jnp.zeros((80, 128), f32)

    def everyone(f):
        def step(i, _):
            tx = lax.rem(x + lax.div(i, 4), 4)
            ty = lax.rem(yy + lax.rem(i, 4), 4)
            for dc in range(2):
                for dz in range(4):
                    to = (tx, ty, lax.rem(c + dc, 2), lax.rem(z + dz, 4))
                    if dc == 0 and dz == 0:
                        pl.when(i > 0)(lambda to=to: f(to))
                    else:
                        f(to)
            return 0

        lax.fori_loop(0, 16, step, 0)

    barrier = pltpu.get_barrier_semaphore()
    everyone(lambda to: pl.semaphore_signal(barrier, inc=1, device_id=to, device_id_type=MESH))

    slot = lax.broadcasted_iota(i32, (LINES, 128), 0) * 128 + lax.broadcasted_iota(i32, (LINES, 128), 1)
    w[...] = jnp.where(slot < count[0, 0], prec[...], 0.0)
    y[...] = w[...] * innov[...]

    iota_s = lax.broadcasted_iota(i32, (128, 128), 0)
    iota_l = lax.broadcasted_iota(i32, (128, 128), 1)

    def count_of(m, v=1):
        return sum8(jnp.where(m, v, 0))

    a = jnp.broadcast_to(col[:, 0:1] >> 6, (128, 128))
    row_l = count_of(iota_s == iota_l, a)
    b = bc(row_l, 128)
    rank = jnp.transpose(bc(count_of((a < b) | ((a == b) & (iota_s < iota_l))), 128))
    put = rank == iota_l
    iv[0:1] = count_of(put, iota_s)
    iv[1:2] = count_of(put, a)
    iv[2:3] = jnp.maximum(count_of(a <= iota_l) - 1, 0)
    iv[3:4] = count_of(a == iota_l)
    iv[4:5] = row_l
    iv[5:8] = jnp.zeros((3, 128), i32)
    to_smem = pltpu.make_async_copy(iv, sm_i, s_load.at[1])
    to_smem.start()
    make_hot(chan, oh)
    cl[...] = col[...] & 63

    for i in range(8):
        ob[i] = jnp.zeros((8, 128), f32)

    def scatter(send, recv, ph):
        def step(i, _):
            tz = lax.rem(z + lax.div(i, 10), 4)
            j = lax.rem(s + lax.rem(i, 10), 10)
            t = tz * 10 + j
            to = coords(3 * j) + (tz,)

            @pl.when((3 * j != s) | (tz != z))
            def _():
                pltpu.make_async_remote_copy(
                    src_ref=send.at[t], dst_ref=recv.at[me], send_sem=s_rs_s.at[ph],
                    recv_sem=s_rs_r.at[ph], device_id=to, device_id_type=MESH,
                ).start()

            return 0

        lax.fori_loop(0, TILES, step, 0, unroll=4)

        @pl.when(owner)
        def _():
            recv[me] = send[mine]

    def gathered(recv, ph):
        wait_all(recv.at[pl.ds(0, 127)], s_rs_r.at[ph])
        total = recv[0]
        for i in range(1, 128):
            total += recv[i]
        return total

    def spread(k):
        def send(to):
            pltpu.make_async_remote_copy(
                src_ref=zt.at[k, mine], dst_ref=zt.at[k, mine], send_sem=s_ag_s.at[k],
                recv_sem=s_ag_r.at[k], device_id=to, device_id_type=MESH,
            ).start()

        everyone(send)

    def wait_spread(k):
        @pl.when(owner)
        def _():
            wait_all(zt.at[k, pl.ds(0, TILES - 1)], s_ag_r.at[k])

        @pl.when(jnp.logical_not(owner))
        def _():
            wait_all(zt.at[k], s_ag_r.at[k])

    def scalars_a(ph, rows):
        n = len(rows)
        mya = c * 4 + z
        sca[ph, mya] = jnp.concatenate(list(rows) + [jnp.zeros((8 - n, 128), f32)], axis=0)
        for d in range(1, 8):
            to = (x, yy, lax.rem(c + d // 4, 2), lax.rem(z + d % 4, 4))
            pltpu.make_async_remote_copy(
                src_ref=sca.at[ph, mya], dst_ref=sca.at[ph, mya], send_sem=s_sc_s.at[ph, 0],
                recv_sem=s_sc_r.at[ph, 0], device_id=to, device_id_type=MESH,
            ).start()

    def scalars_b(ph):
        wait_all(sca.at[ph, pl.ds(0, 7)], s_sc_r.at[ph, 0])
        total = sca[ph, 0]
        for i in range(1, 8):
            total += sca[ph, i]
        myb = x * 4 + yy
        scb[ph, myb] = total
        for d in range(1, 16):
            to = (lax.rem(x + d // 4, 4), lax.rem(yy + d % 4, 4), c, z)
            pltpu.make_async_remote_copy(
                src_ref=scb.at[ph, myb], dst_ref=scb.at[ph, myb], send_sem=s_sc_s.at[ph, 1],
                recv_sem=s_sc_r.at[ph, 1], device_id=to, device_id_type=MESH,
            ).start()

    def scalars_c(ph):
        wait_all(scb.at[ph, pl.ds(0, 15)], s_sc_r.at[ph, 1])
        total = scb[ph, 0]
        for i in range(1, 16):
            total += scb[ph, i]
        sums = jnp.sum(total, axis=1, keepdims=True)
        return sums[0:1], sums[1:2], sums[2:3]

    above, below = coords(s - 1), coords(s + 1)
    left, right = lax.rem(z + 3, 4), lax.rem(z + 1, 4)
    has_above, has_below = s > 0, s < 31

    def halo_copies(ph):
        def mk(n, src, dst, to):
            return pltpu.make_async_remote_copy(
                src_ref=src, dst_ref=dst, send_sem=s_halo_s.at[ph, n],
                recv_sem=s_halo_r.at[ph, n], device_id=to, device_id_type=MESH,
            )

        g = gp.at[ph]
        mid = pl.ds(8, LON)
        sides = [
            mk(0, est.at[ph, 0], hcol.at[ph, 1], (x, yy, c, left)),
            mk(1, est.at[ph, 1], hcol.at[ph, 0], (x, yy, c, right)),
        ]
        up = [
            mk(2, g.at[pl.ds(2, 2), mid], g.at[pl.ds(34, 2), mid], above + (z,)),
            mk(3, g.at[2, pl.ds(8, 8)], cn.at[ph, 0], above + (left,)),
            mk(4, g.at[2, pl.ds(64, 8)], cn.at[ph, 1], above + (right,)),
        ]
        down = [
            mk(5, g.at[pl.ds(32, 2), mid], g.at[pl.ds(0, 2), mid], below + (z,)),
            mk(6, g.at[33, pl.ds(8, 8)], cn.at[ph, 2], below + (left,)),
            mk(7, g.at[33, pl.ds(64, 8)], cn.at[ph, 3], below + (right,)),
        ]
        return sides, up, down

    def halo_send(ph):
        for r in range(LAT):
            g = jnp.where(sm_i[3, r] > 0, seg[sm_i[2, r]], 0.0)
            gp[ph, r + 2, 8:72, :] = g
            est[ph, 0, 2 * r : 2 * r + 2, :] = g[0:2]
            est[ph, 1, 2 * r : 2 * r + 2, :] = g[62:64]
        sides, up, down = halo_copies(ph)
        for cp in sides:
            cp.start()

        @pl.when(has_above)
        def _():
            for cp in up:
                cp.start()

        @pl.when(has_below)
        def _():
            for cp in down:
                cp.start()

    def halo_wait(ph):
        sides, up, down = halo_copies(ph)
        for cp in sides:
            cp.wait_recv()

        @pl.when(has_below)
        def _():
            for cp in up:
                cp.wait_recv()
            gp[ph, 34, 72:73, :] = cn[ph, 0, 0:1]
            gp[ph, 34, 7:8, :] = cn[ph, 1, 7:8]

        @pl.when(has_above)
        def _():
            for cp in down:
                cp.wait_recv()
            gp[ph, 1, 72:73, :] = cn[ph, 2, 0:1]
            gp[ph, 1, 7:8, :] = cn[ph, 3, 7:8]

        for r in range(LAT):
            gp[ph, r + 2, 72:74, :] = hcol[ph, 1, 2 * r : 2 * r + 2]
            gp[ph, r + 2, 6:8, :] = hcol[ph, 0, 2 * r : 2 * r + 2]

    def halo_done(ph):
        sides, up, down = halo_copies(ph)
        for cp in sides:
            cp.wait_send()

        @pl.when(has_above)
        def _():
            for cp in up:
                cp.wait_send()

        @pl.when(has_below)
        def _():
            for cp in down:
                cp.wait_send()

    sm = smooth[...]

    def smoothed(ref, r):
        v = ref[r]
        beside = ref[r - 1] + ref[r + 1] + pltpu.roll(v, 1, 0) + pltpu.roll(v, 79, 0)
        return v + sm * (beside - 4.0 * v)

    def inside(r):
        return ((r > 1) | has_above) & ((r < 34) | has_below)

    def squares(v):
        v = v * v
        t = v[0:8]
        for i in range(1, LON // 8):
            t += v[8 * i : 8 * i + 8]
        return t

    def to_forward(src):
        def step(r, total):
            u = smoothed(src, r)[8:72]
            hi, lo = split(u)
            u2[r - 2, 0:LON] = hi
            u2[r - 2, LON : 2 * LON] = lo
            return total + squares(src[r, 8:72, :])

        return sum8(lax.fori_loop(2, 34, step, jnp.zeros((8, 128), f32)))

    def slots_of(k):
        wait_spread(k)
        lookup(zt.at[k], chan, pred, pc)
        image = hs[...] + pc[...]
        yw = w[...] * image
        y[...] = yw
        return sum8(yw * image)

    def term_y(b):
        return pred[:, lanes(b)] * y[pl.ds(b, 1), :]

    def term_d(b):
        p = pred[:, lanes(b)]
        return p * p * w[pl.ds(b, 1), :]

    bias_adjoint([term_y, term_d], chan, oh, lhs, acc)
    for t in range(TILES):
        rs0_send[t, 0:8] = acc_tile(acc, 0, t)
        rs0_send[t, 8:16] = acc_tile(acc, 1, t)
    pl.semaphore_wait(barrier, 127)
    scatter(rs0_send, rs0_recv, 0)
    to_smem.wait()
    load_j.wait()
    adjoint(y, jac, sm_i, cl, seg)
    halo_send(0)

    @pl.when(owner)
    def _():
        both = gathered(rs0_recv, 0)
        bp = biasp[:, lanes(lax.div(s, 3))]
        rb, dg = both[0:8], both[8:16] + bp
        zb = rb / dg
        ob[0] = rb
        ob[1] = dg
        ob[2] = zb
        ob[3] = bp
        zt[0, mine] = zb
        spread(0)

    halo_wait(0)

    def first(r, _):
        r0[r] = jnp.where(inside(r), smoothed(gp.at[0], r), 0.0)
        return 0

    lax.fori_loop(1, 35, first, 0)
    rr_state = to_forward(r0)

    forward(u2, jac, sm_i, cl, hs)
    d0 = slots_of(0)
    scalars_a(0, (
        rr_state + sum8(ob[0] * ob[2]),
        rr_state + d0 + sum8(ob[3] * ob[2] * ob[2]),
        rr_state + sum8(ob[0] * ob[0]),
    ))
    bias_adjoint([term_y], chan, oh, lhs, acc)
    for t in range(TILES):
        rs_send[0, t] = acc_tile(acc, 0, t)
    scatter(rs_send.at[0], rs_recv.at[0], 1)
    scalars_b(0)
    adjoint(y, jac, sm_i, cl, seg)
    halo_send(1)
    rz0, pq0, rr0 = scalars_c(0)
    alpha0 = rz0 / pq0

    @pl.when(owner)
    def _():
        qb = ob[3] * ob[2] + gathered(rs_recv.at[0], 1)
        rb = ob[0] - alpha0 * qb
        zb = rb / ob[1]
        ob[4] = qb
        ob[5] = rb
        ob[6] = zb
        zt[1, mine] = zb
        spread(1)

    halo_wait(1)

    def second(r, _):
        q = r0[r] + jnp.where(inside(r), smoothed(gp.at[1], r), 0.0)
        q0[r] = q
        r1[r] = r0[r] - alpha0 * q
        return 0

    lax.fori_loop(1, 35, second, 0)
    rr_state = to_forward(r1)

    forward(u2, jac, sm_i, cl, hs)
    d1 = slots_of(1)
    scalars_a(1, (
        rr_state + sum8(ob[5] * ob[6]),
        rr_state + d1 + sum8(ob[3] * ob[6] * ob[6]),
        rr_state + sum8(ob[5] * ob[5]),
    ))
    bias_adjoint([term_y], chan, oh, lhs, acc)
    for t in range(TILES):
        rs_send[1, t] = acc_tile(acc, 0, t)
    scatter(rs_send.at[1], rs_recv.at[1], 2)
    scalars_b(1)
    adjoint(y, jac, sm_i, cl, seg)
    halo_send(2)
    rz1, zaz, rr1 = scalars_c(1)
    beta = rz1 / rz0
    alpha1 = rz1 / (zaz - beta * rz1 / alpha0)
    mix = alpha0 + alpha1 * beta

    def solved(r, _):
        xs[r - 2] = mix * r0[r, 8:72, :] + alpha1 * r1[r, 8:72, :]
        return 0

    lax.fori_loop(2, 34, solved, 0)
    store_x = pltpu.make_async_copy(xs, out_x, s_load.at[2])
    store_x.start()
    for t in range(10):
        at = z * 10 + t
        out_b[:, t * 128 : (t + 1) * 128] = mix * zt[0, at] + alpha1 * zt[1, at]

    @pl.when(owner)
    def _():
        qb = ob[3] * ob[6] + gathered(rs_recv.at[1], 2) + beta * ob[4]
        ob[7] = ob[5] - alpha1 * qb

    halo_wait(2)

    def last(r, total):
        v = r1[r, 8:72, :]
        q = v + smoothed(gp.at[2], r)[8:72] + beta * q0[r, 8:72, :]
        return total + squares(v - alpha1 * q)

    rr_state = sum8(lax.fori_loop(2, 34, last, jnp.zeros((8, 128), f32)))
    scalars_a(2, (rr_state + sum8(ob[7] * ob[7]),))
    scalars_b(2)
    rr2, _, _ = scalars_c(2)
    lane = lax.broadcasted_iota(i32, (1, 128), 1)
    out_n[...] = jnp.sqrt(jnp.where(lane == 0, rr0, jnp.where(lane == 1, rr1, rr2)))

    for ph, ref in ((0, rs0_send), (1, rs_send.at[0]), (2, rs_send.at[1])):
        @pl.when(owner)
        def _(ph=ph, ref=ref):
            wait_all(ref.at[pl.ds(0, TILES - 1)], s_rs_s.at[ph])

        @pl.when(jnp.logical_not(owner))
        def _(ph=ph, ref=ref):
            wait_all(ref, s_rs_s.at[ph])

    @pl.when(owner)
    def _():
        for k in range(2):
            wait_all(rs_recv.at[0, pl.ds(0, 127)], s_ag_s.at[k])

    for ph in range(3):
        halo_done(ph)
        wait_all(sca.at[ph, pl.ds(0, 7)], s_sc_s.at[ph, 0])
        wait_all(scb.at[ph, pl.ds(0, 15)], s_sc_s.at[ph, 1])
    store_x.wait()


def body(innovations, obs_precision, jacobian, predictors, obs_column, obs_channel, obs_count, smoothing, bias_precision):
    vm = pl.BlockSpec(memory_space=pltpu.VMEM)
    hbm = pl.BlockSpec(memory_space=pl.ANY)
    sq = (LINES, 128)
    V = pltpu.VMEM
    D = pltpu.SemaphoreType.DMA
    out = pl.pallas_call(
        kernel,
        name="pcg",
        out_shape=(
            jax.ShapeDtypeStruct((LAT, LON, LEV), f32),
            jax.ShapeDtypeStruct((NPRED, 1280), f32),
            jax.ShapeDtypeStruct((1, 128), f32),
        ),
        in_specs=[vm, vm, hbm, vm, vm, vm, pl.BlockSpec(memory_space=pltpu.SMEM), vm, vm],
        out_specs=(hbm, vm, vm),
        scratch_shapes=[
            V((LINES, 128, LEV), bf16), V((256, 16384), bf16), V((640, KL * 128), bf16), V((640, 256), f32),
            V(sq, f32), V(sq, f32), V(sq, f32), V(sq, f32),
            V((LAT, 2 * LON, LEV), bf16), V((LINES, LON, LEV), f32),
            V((3, 36, 80, LEV), f32), V((36, 80, LEV), f32), V((36, 80, LEV), f32), V((36, 80, LEV), f32),
            V((LAT, LON, LEV), f32), V((3, 2, 64, LEV), f32), V((3, 2, 64, LEV), f32), V((3, 4, 8, LEV), f32),
            V((TILES, 16, 128), f32), V((128, 16, 128), f32), V((2, TILES, 8, 128), f32), V((2, 128, 8, 128), f32),
            V((2, TILES, 8, 128), f32), V((3, 8, 8, 128), f32), V((3, 16, 8, 128), f32), V((8, 8, 128), f32),
            V((8, 128), i32), V(sq, i32), pltpu.SMEM((8, 128), i32),
            D((3,)), D((3, 8)), D((3, 8)), D((3,)), D((3,)), D((2,)), D((2,)), D((3, 2)), D((3, 2)),
        ],
        compiler_params=pltpu.CompilerParams(
            collective_id=0, has_side_effects=True, vmem_limit_bytes=62 * 2**20
        ),
    )(
        innovations.reshape(sq), obs_precision.reshape(sq), jacobian.reshape(LINES, 128, LEV), predictors,
        obs_column.reshape(sq), obs_channel.reshape(sq), obs_count, smoothing.reshape(1, LEV), bias_precision,
    )
    return out[0], out[1], out[2][0, :3]


def solution(mesh):
    torus = Mesh(mesh.devices.reshape(4, 4, 2, mesh.shape["chan"]), AX)
    placed = (
        P(AX), P(AX), P(AX, None), P(None, AX), P(AX), P(AX), P(SWATH, "chan"), P(), P(None, "chan"),
    )
    return jax.shard_map(
        body,
        mesh=torus,
        in_specs=placed,
        out_specs=(P(SWATH, "chan", None), P(None, "chan"), P()),
        check_vma=False,
    )
```

profile of v0, /device:TPU:0, one launch (start us, length us, event | category | flops | bytes accessed | tf_op | source)
XLA Modules:
  0.0 107.3 jit_solution(643552733466061994)
XLA Ops:
  1.3 101.2 %pcg.1 = (f32[32,64,128]{2,1,0:T(8,128)}, f32[8,1280]{1,0:T(8,128)}, f32[1,128]{1,0:T(1,128)}) custom-call(f32[128,128]{1,0:T(8,128)} %bitcast.9, f32[128,128]{1,0:T(8,128)} %bitcast.10, bf16[128,128,128]{2,1,0:T(8,128)(2,1)} %bitcast.8, f32[8,16384]{1,0:T(8,128)} %pred_.1, s32[128,128]{1,0:T(8,128)} %bitcast.11, s32[128,128]{1,0:T(8,128)} %bitcast.12, ...), custom_call_target="tpu_custom_call" | custom-call | tf_op jit(solution)/shard_map/pcg/pallas_call | solution.py:564
  102.5 1.1 %slice_bitcast_fusion = f32[3]{0:T(128)} fusion(f32[1,128]{1,0:T(1,128)} %get-tuple-element.8), kind=kLoop, calls=%fused_computation | loop fusion | bytes 24 | tf_op jit(solution)/shard_map/squeeze | solution.py:592
  103.6 2.3 %copy.15 = f32[32,64,128]{2,1,0:T(8,128)} copy(f32[32,64,128]{2,1,0:T(8,128)} %get-tuple-element.12) | data formatting | bytes 2097152
  105.9 1.4 %copy.16 = f32[8,1280]{1,0:T(8,128)} copy(f32[8,1280]{1,0:T(8,128)} %get-tuple-element.13) | data formatting | bytes 81920
where the time goes:
time: 108 us; the launch traced here: 107 us
  Pallas kernels  101 us (94%)
  local copies, waits for them, and re-layouts  4.79 us (4%)
  between operations  1.29 us (1%)
    pallas_call x1, Pallas kernels, body(): pl.pallas_call(kernel, name='pcg', out_shape=(jax.ShapeDtypeStruct((LAT,...  101 us
    unnamed x2, local copies, waits for them, and re-layouts  3.7 us

commit v1 on v0

--- a/solution.py
+++ b/solution.py
@@ -17,8 +17,8 @@
 MESH = pl.DeviceIdType.MESH
 NT = (((1,), (1,)), ((), ()))
 bf16, f32, i32 = jnp.bfloat16, jnp.float32, jnp.int32
-KL = 8
-UN = 8
+KL = 32
+UN = 32
 
 
 def split(t):
@@ -38,17 +38,28 @@
     return jnp.sum(x, axis=0, keepdims=True)
 
 
-def lookup(tab, ch_ref, pred_ref, out_ref):
+def make_table(zt, tab):
+    for h in range(20):
+        t = jnp.concatenate([zt[2 * h], zt[2 * h + 1]], axis=1)
+        tab[16 * h : 16 * h + 16] = jnp.concatenate(split(t), axis=0)
+
+
+def lookup(tab, oh, ch_ref, pred_ref, out_ref):
     def step(i, _):
-        for u in range(UN):
-            b = i * UN + u
-            ch = bc(ch_ref[pl.ds(b, 1), :], 8)
-            lo, hi = ch & 127, ch >> 7
-            acc = jnp.zeros((8, 128), f32)
-            for h in range(TILES):
-                g = jnp.take_along_axis(tab[h], lo, axis=1, mode="promise_in_bounds")
-                acc = jnp.where(hi == h, g, acc)
-            out_ref[pl.ds(b, 1), :] = sum8(acc * pred_ref[:, lanes(b)])
+        for g in range(UN // 2):
+            b0 = i * UN + 2 * g
+            hot = jnp.concatenate([oh[b0], oh[b0 + 1]], axis=1)
+            got = jnp.dot(tab[...], hot, preferred_element_type=f32)
+            for u in range(2):
+                b, ls = b0 + u, slice(u * 128, u * 128 + 128)
+                hb = bc(ch_ref[pl.ds(b, 1), :] >> 8, 8)
+                hi = jnp.zeros((8, 128), f32)
+                lo = hi
+                for h in range(20):
+                    m = hb == h
+                    hi = jnp.where(m, got[16 * h : 16 * h + 8, ls], hi)
+                    lo = jnp.where(m, got[16 * h + 8 : 16 * h + 16, ls], lo)
+                out_ref[pl.ds(b, 1), :] = sum8((hi + lo) * pred_ref[:, lanes(b)])
         return 0
 
     lax.fori_loop(0, LINES // UN, step, 0)
@@ -92,38 +103,42 @@
 
 
 def make_hot(ch_ref, oh):
-    iota = lax.broadcasted_iota(i32, (256, 128), 0)
-
-    def step(b, _):
-        ch = ch_ref[pl.ds(b, 1), :] & 255
-        oh[:, lanes(b)] = jnp.where(iota == bc(ch, 256), 1.0, 0.0).astype(bf16)
+    iota = lax.broadcasted_iota(i32, (256, 128), 0).astype(f32).astype(bf16)
+    one, zero = jnp.ones((), bf16), jnp.zeros((), bf16)
+
+    def step(i, _):
+        for u in range(8):
+            b = i * 8 + u
+            ch = bc((ch_ref[pl.ds(b, 1), :] & 255).astype(f32), 16).astype(bf16)
+            for j in range(0, 256, 16):
+                oh[b, j : j + 16] = jnp.where(iota[j : j + 16] == ch, one, zero)
         return 0
 
-    lax.fori_loop(0, LINES, step, 0)
+    lax.fori_loop(0, LINES // 8, step, 0)
 
 
 def bias_adjoint(terms, ch_ref, oh, lhs, acc):
-    rows, k = 320 * len(terms), KL * 128
+    n = len(terms)
+    rows, kl = 320 * n, KL // n
+    zero = jnp.zeros((), bf16)
 
     def step(c, _):
-        for l in range(KL):
-            b = c * KL + l
+        for l in range(kl):
+            b = c * kl + l
             hb = bc((ch_ref[pl.ds(b, 1), :] >> 8).astype(f32), 16).astype(bf16)
-            for j, f in enumerate(terms):
-                st = jnp.concatenate(split(f(b)), axis=0)
-                for h in range(20):
+            sts = [jnp.concatenate(split(f(b)), axis=0) for f in terms]
+            for h in range(20):
+                m = hb == jnp.asarray(h, bf16)
+                for j, st in enumerate(sts):
                     at = (j * 20 + h) * 16
-                    lhs[at : at + 16, l * 128 : (l + 1) * 128] = jnp.where(
-                        hb == jnp.asarray(h, bf16), st, jnp.zeros((), bf16)
-                    )
-        part = lax.dot_general(
-            lhs[:rows], oh[:, pl.ds(pl.multiple_of(c * k, k), k)], NT, preferred_element_type=f32
-        )
-        acc[:rows] += part
+                    lhs[l, at : at + 16] = jnp.where(m, st, zero)
+        left = jnp.concatenate([lhs[l, :rows] for l in range(kl)], axis=1)
+        hot = jnp.concatenate([oh[c * kl + l] for l in range(kl)], axis=1)
+        acc[:rows] += lax.dot_general(left, hot, NT, preferred_element_type=f32)
         return 0
 
     acc[:rows] = jnp.zeros((rows, 256), f32)
-    lax.fori_loop(0, LINES // KL, step, 0)
+    lax.fori_loop(0, LINES // kl, step, 0)
 
 
 def acc_tile(acc, j, t):
@@ -138,7 +153,7 @@
 def kernel(
     innov, prec, jac_hbm, pred, col, chan, count, smooth, biasp,
     out_x, out_b, out_n,
-    jac, oh, lhs, acc, w, y, hs, pc, u2, seg, gp, r0, r1, q0, xs, est, hcol, cn,
+    jac, oh, lhs, acc, tab, w, y, hs, pc, u2, seg, gp, r0, r1, q0, xs, est, hcol, cn,
     rs0_send, rs0_recv, rs_send, rs_recv, zt, sca, scb, ob, iv, cl, sm_i,
     s_load, s_halo_s, s_halo_r, s_rs_s, s_rs_r, s_ag_s, s_ag_r, s_sc_s, s_sc_r,
 ):
@@ -400,7 +415,8 @@
 
     def slots_of(k):
         wait_spread(k)
-        lookup(zt.at[k], chan, pred, pc)
+        make_table(zt.at[k], tab)
+        lookup(tab, oh, chan, pred, pc)
         image = hs[...] + pc[...]
         yw = w[...] * image
         y[...] = yw
@@ -572,7 +588,7 @@
         in_specs=[vm, vm, hbm, vm, vm, vm, pl.BlockSpec(memory_space=pltpu.SMEM), vm, vm],
         out_specs=(hbm, vm, vm),
         scratch_shapes=[
-            V((LINES, 128, LEV), bf16), V((256, 16384), bf16), V((640, KL * 128), bf16), V((640, 256), f32),
+            V((LINES, 128, LEV), bf16), V((LINES, 256, 128), bf16), V((KL, 640, 128), bf16), V((640, 256), f32), V((320, 256), bf16),
             V(sq, f32), V(sq, f32), V(sq, f32), V(sq, f32),
             V((LAT, 2 * LON, LEV), bf16), V((LINES, LON, LEV), f32),
             V((3, 36, 80, LEV), f32), V((36, 80, LEV), f32), V((36, 80, LEV), f32), V((36, 80, LEV), f32),

time: 108 us -> 90.5 us (0.84)
  Pallas kernels: 101 us -> 84 us
    pallas_call x1, Pallas kernels: 101 us -> 84 us  [body(): pl.pallas_call(kernel, name='pcg', out_shape=(jax.ShapeDtypeStruct((LAT,...]
where the time goes in v1:
time: 90.5 us; the launch traced here: 90.1 us
  Pallas kernels  84 us (93%)
  local copies, waits for them, and re-layouts  4.79 us (5%)
  between operations  1.29 us (1%)
    pallas_call x1, Pallas kernels, body(): pl.pallas_call(kernel, name='pcg', out_shape=(jax.ShapeDtypeStruct((LAT,...  84 us
    unnamed x2, local copies, waits for them, and re-layouts  3.7 us

profile of v1, /device:TPU:0, one launch (start us, length us, event | category | flops | bytes accessed | tf_op | source)
XLA Modules:
  0.0 90.1 jit_solution(2652031729346521125)
XLA Ops:
  1.3 84.0 %pcg.1 = (f32[32,64,128]{2,1,0:T(8,128)}, f32[8,1280]{1,0:T(8,128)}, f32[1,128]{1,0:T(1,128)}) custom-call(f32[128,128]{1,0:T(8,128)} %bitcast.9, f32[128,128]{1,0:T(8,128)} %bitcast.10, bf16[128,128,128]{2,1,0:T(8,128)(2,1)} %bitcast.8, f32[8,16384]{1,0:T(8,128)} %pred_.1, s32[128,128]{1,0:T(8,128)} %bitcast.11, s32[128,128]{1,0:T(8,128)} %bitcast.12, ...), custom_call_target="tpu_custom_call" | custom-call | tf_op jit(solution)/shard_map/pcg/pallas_call | solution.py:580
  85.3 1.1 %slice_bitcast_fusion = f32[3]{0:T(128)} fusion(f32[1,128]{1,0:T(1,128)} %get-tuple-element.8), kind=kLoop, calls=%fused_computation | loop fusion | bytes 24 | tf_op jit(solution)/shard_map/squeeze | solution.py:608
  86.4 2.3 %copy.15 = f32[32,64,128]{2,1,0:T(8,128)} copy(f32[32,64,128]{2,1,0:T(8,128)} %get-tuple-element.12) | data formatting | bytes 2097152
  88.7 1.4 %copy.16 = f32[8,1280]{1,0:T(8,128)} copy(f32[8,1280]{1,0:T(8,128)} %get-tuple-element.13) | data formatting | bytes 81920

commit v2 on v1

--- a/solution.py
+++ b/solution.py
@@ -19,6 +19,7 @@
 bf16, f32, i32 = jnp.bfloat16, jnp.float32, jnp.int32
 KL = 32
 UN = 32
+PIECES = 4
 
 
 def split(t):
@@ -38,9 +39,14 @@
     return jnp.sum(x, axis=0, keepdims=True)
 
 
+def place(t):
+    j = t % 10
+    return (j % 2) * 20 + (t // 10) * 5 + j // 2
+
+
 def make_table(zt, tab):
     for h in range(20):
-        t = jnp.concatenate([zt[2 * h], zt[2 * h + 1]], axis=1)
+        t = jnp.concatenate([zt[place(2 * h)], zt[place(2 * h + 1)]], axis=1)
         tab[16 * h : 16 * h + 16] = jnp.concatenate(split(t), axis=0)
 
 
@@ -69,12 +75,16 @@
     iota = lax.broadcasted_iota(i32, (LON, 128), 0)
 
     def step(i, _):
-        for u in range(UN):
-            b = i * UN + u
-            both = lax.dot_general(u2[sm_i[4, b]], jac[b], NT, preferred_element_type=f32)
-            s = both[:LON] + both[LON:]
-            m = iota == bc(col_ref[pl.ds(b, 1), :], LON)
-            out_ref[pl.ds(b, 1), :] = sum8(jnp.where(m, s, 0.0))
+        for g in range(UN // 2):
+            b0 = i * UN + 2 * g
+            left = jnp.concatenate([u2[sm_i[4, b0]], u2[sm_i[4, b0 + 1]]], axis=0)
+            pair = jnp.concatenate([jac[b0], jac[b0 + 1]], axis=0)
+            both = lax.dot_general(left, pair, NT, preferred_element_type=f32)
+            for u in range(2):
+                b, at = b0 + u, 128 * u
+                mine = both[at : at + 128, at : at + 128]
+                m = iota == bc(col_ref[pl.ds(b, 1), :], LON)
+                out_ref[pl.ds(b, 1), :] = sum8(jnp.where(m, mine[:LON] + mine[LON:], 0.0))
         return 0
 
     lax.fori_loop(0, LINES // UN, step, 0)
@@ -151,45 +161,62 @@
 
 
 def kernel(
-    innov, prec, jac_hbm, pred, col, chan, count, smooth, biasp,
+    innov_hbm, prec_hbm, jac_hbm, pred_hbm, col_hbm, chan_hbm, count, smooth_hbm, biasp_hbm,
     out_x, out_b, out_n,
-    jac, oh, lhs, acc, tab, w, y, hs, pc, u2, seg, gp, r0, r1, q0, xs, est, hcol, cn,
-    rs0_send, rs0_recv, rs_send, rs_recv, zt, sca, scb, ob, iv, cl, sm_i,
-    s_load, s_halo_s, s_halo_r, s_rs_s, s_rs_r, s_ag_s, s_ag_r, s_sc_s, s_sc_r,
+    innov, prec, pred, col, chan, smooth, biasp, jac, oh, lhs, acc, tab, w, y, hs, pc, u2, seg, gp, r0, r1, q0, xs, est, hcol, cn,
+    rs0_send, pr0, rs0_recv, rs_send, pr, rs_recv, zt, sp, sc, ob, iv, cl, sm_i,
+    s_load, s_halo_s, s_halo_r, s_pr_s, s_pr_r, s_rs_s, s_rs_r, s_ag_s, s_ag_r, s_rl_s, s_rl_r,
+    s_sp_s, s_sp_r, s_sc_s, s_sc_r,
 ):
     x, yy, c, z = (lax.axis_index(a) for a in AX)
     s = (x * 4 + yy) * 2 + c
     owner = (lax.rem(s, 3) == 0) & (s < 30)
-    mine = z * 10 + lax.div(s, 3)
-    me = s * 4 + z
+    half = c * 20
+    mine = half + z * 5 + lax.div(s, 6)
+    chip = (x * 4 + yy) * 4 + z
+    partner = (x, yy, 1 - c, z)
+    xs4 = [lax.rem(x + d, 4) for d in range(4)]
+    ys4 = [lax.rem(yy + d, 4) for d in range(4)]
+    zs4 = [lax.rem(z + d, 4) for d in range(4)]
 
     def coords(sw):
         return lax.div(sw, 8), lax.rem(lax.div(sw, 2), 4), lax.rem(sw, 2)
 
-    load_j = pltpu.make_async_copy(jac_hbm, jac, s_load.at[0])
-    load_j.start()
+    pairs = (
+        (innov_hbm, innov), (prec_hbm, prec), (col_hbm, col), (chan_hbm, chan), (pred_hbm, pred),
+        (smooth_hbm, smooth), (biasp_hbm, biasp), (jac_hbm, jac),
+    )
+    loads = [pltpu.make_async_copy(a, b, s_load.at[i]) for i, (a, b) in enumerate(pairs)]
+    for cp in loads:
+        cp.start()
     for ph in range(3):
         for r in (0, 1, 34, 35):
             gp[ph, r] = jnp.zeros((80, 128), f32)
 
-    def everyone(f):
-        def step(i, _):
-            tx = lax.rem(x + lax.div(i, 4), 4)
-            ty = lax.rem(yy + lax.rem(i, 4), 4)
-            for dc in range(2):
-                for dz in range(4):
-                    to = (tx, ty, lax.rem(c + dc, 2), lax.rem(z + dz, 4))
-                    if dc == 0 and dz == 0:
-                        pl.when(i > 0)(lambda to=to: f(to))
-                    else:
-                        f(to)
-            return 0
-
-        lax.fori_loop(0, 16, step, 0)
+    def chips(f):
+        for d in range(1, 64):
+            f((xs4[d // 16], ys4[d // 4 % 4], c, zs4[d % 4]))
+
+    above, below = coords(s - 1), coords(s + 1)
+    left, right = zs4[3], zs4[1]
+    has_above, has_below = s > 0, s < 31
 
     barrier = pltpu.get_barrier_semaphore()
-    everyone(lambda to: pl.semaphore_signal(barrier, inc=1, device_id=to, device_id_type=MESH))
-
+
+    def greet(to):
+        pl.semaphore_signal(barrier, inc=1, device_id=to, device_id_type=MESH)
+
+    chips(greet)
+    for there, side in ((has_above, above), (has_below, below)):
+        @pl.when(there)
+        def _(side=side):
+            for to_z in (z, left, right):
+                greet(side + (to_z,))
+
+    greeted = 63 + jnp.where(has_above, 3, 0) + jnp.where(has_below, 3, 0)
+
+    for cp in loads[:7]:
+        cp.wait()
     slot = lax.broadcasted_iota(i32, (LINES, 128), 0) * 128 + lax.broadcasted_iota(i32, (LINES, 128), 1)
     w[...] = jnp.where(slot < count[0, 0], prec[...], 0.0)
     y[...] = w[...] * innov[...]
@@ -211,7 +238,7 @@
     iv[3:4] = count_of(a == iota_l)
     iv[4:5] = row_l
     iv[5:8] = jnp.zeros((3, 128), i32)
-    to_smem = pltpu.make_async_copy(iv, sm_i, s_load.at[1])
+    to_smem = pltpu.make_async_copy(iv, sm_i, s_load.at[8])
     to_smem.start()
     make_hot(chan, oh)
     cl[...] = col[...] & 63
@@ -219,34 +246,40 @@
     for i in range(8):
         ob[i] = jnp.zeros((8, 128), f32)
 
-    def scatter(send, recv, ph):
-        def step(i, _):
-            tz = lax.rem(z + lax.div(i, 10), 4)
-            j = lax.rem(s + lax.rem(i, 10), 10)
-            t = tz * 10 + j
-            to = coords(3 * j) + (tz,)
-
-            @pl.when((3 * j != s) | (tz != z))
-            def _():
+    def pair_send(send, pair, ph):
+        pltpu.make_async_remote_copy(
+            src_ref=send.at[pl.ds(20 - half, 20)], dst_ref=pair, send_sem=s_pr_s.at[ph],
+            recv_sem=s_pr_r.at[ph], device_id=partner, device_id_type=MESH,
+        ).start()
+
+    def scatter(send, pair, recv, ph):
+        wait_all(pair, s_pr_r.at[ph])
+        for i in range(20):
+            pair[i] = pair[i] + send[half + i]
+        for i in range(20):
+            tz = zs4[i // 5]
+            jj = lax.rem(x + yy + i % 5, 5)
+            sw = 6 * jj + 3 * c
+            tx, ty = lax.div(sw, 8), lax.rem(lax.div(sw, 2), 4)
+            away = (tx != x) | (ty != yy) | (tz != z)
+
+            @pl.when(away)
+            def _(tz=tz, jj=jj, tx=tx, ty=ty):
                 pltpu.make_async_remote_copy(
-                    src_ref=send.at[t], dst_ref=recv.at[me], send_sem=s_rs_s.at[ph],
-                    recv_sem=s_rs_r.at[ph], device_id=to, device_id_type=MESH,
+                    src_ref=pair.at[tz * 5 + jj], dst_ref=recv.at[chip], send_sem=s_rs_s.at[ph],
+                    recv_sem=s_rs_r.at[ph], device_id=(tx, ty, c, tz), device_id_type=MESH,
                 ).start()
 
-            return 0
-
-        lax.fori_loop(0, TILES, step, 0, unroll=4)
-
         @pl.when(owner)
         def _():
-            recv[me] = send[mine]
+            recv[chip] = pair[mine - half]
 
     def gathered(recv, ph):
-        wait_all(recv.at[pl.ds(0, 127)], s_rs_r.at[ph])
-        total = recv[0]
-        for i in range(1, 128):
-            total += recv[i]
-        return total
+        wait_all(recv.at[pl.ds(0, 63)], s_rs_r.at[ph])
+        parts = [recv[i] for i in range(4)]
+        for i in range(4, 64):
+            parts[i % 4] += recv[i]
+        return (parts[0] + parts[1]) + (parts[2] + parts[3])
 
     def spread(k):
         def send(to):
@@ -255,53 +288,61 @@
                 recv_sem=s_ag_r.at[k], device_id=to, device_id_type=MESH,
             ).start()
 
-        everyone(send)
+        chips(send)
+
+    def relay(k):
+        ours = zt.at[k, pl.ds(half, 20)]
+        return pltpu.make_async_remote_copy(
+            src_ref=ours, dst_ref=ours, send_sem=s_rl_s.at[k], recv_sem=s_rl_r.at[k],
+            device_id=partner, device_id_type=MESH,
+        )
 
     def wait_spread(k):
         @pl.when(owner)
         def _():
-            wait_all(zt.at[k, pl.ds(0, TILES - 1)], s_ag_r.at[k])
+            wait_all(zt.at[k, pl.ds(0, 19)], s_ag_r.at[k])
 
         @pl.when(jnp.logical_not(owner))
         def _():
-            wait_all(zt.at[k], s_ag_r.at[k])
+            wait_all(zt.at[k, pl.ds(0, 20)], s_ag_r.at[k])
+
+        relay(k).start()
+        wait_all(zt.at[k, pl.ds(0, 20)], s_rl_r.at[k])
+
+    lane = lax.broadcasted_iota(i32, (1, 128), 1)
+
+    def scalar_pair(ph):
+        return pltpu.make_async_remote_copy(
+            src_ref=sp.at[ph, 0], dst_ref=sp.at[ph, 1], send_sem=s_sp_s.at[ph],
+            recv_sem=s_sp_r.at[ph], device_id=partner, device_id_type=MESH,
+        )
 
     def scalars_a(ph, rows):
-        n = len(rows)
-        mya = c * 4 + z
-        sca[ph, mya] = jnp.concatenate(list(rows) + [jnp.zeros((8 - n, 128), f32)], axis=0)
-        for d in range(1, 8):
-            to = (x, yy, lax.rem(c + d // 4, 2), lax.rem(z + d % 4, 4))
+        row = jnp.zeros((1, 128), f32)
+        for i, r in enumerate(rows):
+            row = jnp.where(lane == i, jnp.sum(r, axis=1, keepdims=True), row)
+        sp[ph, 0] = row
+        scalar_pair(ph).start()
+
+    def scalars_b(ph):
+        scalar_pair(ph).wait_recv()
+        sc[ph, chip] = sp[ph, 0] + sp[ph, 1]
+
+        def send(to):
             pltpu.make_async_remote_copy(
-                src_ref=sca.at[ph, mya], dst_ref=sca.at[ph, mya], send_sem=s_sc_s.at[ph, 0],
-                recv_sem=s_sc_r.at[ph, 0], device_id=to, device_id_type=MESH,
+                src_ref=sc.at[ph, chip], dst_ref=sc.at[ph, chip], send_sem=s_sc_s.at[ph],
+                recv_sem=s_sc_r.at[ph], device_id=to, device_id_type=MESH,
             ).start()
 
-    def scalars_b(ph):
-        wait_all(sca.at[ph, pl.ds(0, 7)], s_sc_r.at[ph, 0])
-        total = sca[ph, 0]
-        for i in range(1, 8):
-            total += sca[ph, i]
-        myb = x * 4 + yy
-        scb[ph, myb] = total
-        for d in range(1, 16):
-            to = (lax.rem(x + d // 4, 4), lax.rem(yy + d % 4, 4), c, z)
-            pltpu.make_async_remote_copy(
-                src_ref=scb.at[ph, myb], dst_ref=scb.at[ph, myb], send_sem=s_sc_s.at[ph, 1],
-                recv_sem=s_sc_r.at[ph, 1], device_id=to, device_id_type=MESH,
-            ).start()
+        chips(send)
 
     def scalars_c(ph):
-        wait_all(scb.at[ph, pl.ds(0, 15)], s_sc_r.at[ph, 1])
-        total = scb[ph, 0]
-        for i in range(1, 16):
-            total += scb[ph, i]
-        sums = jnp.sum(total, axis=1, keepdims=True)
-        return sums[0:1], sums[1:2], sums[2:3]
-
-    above, below = coords(s - 1), coords(s + 1)
-    left, right = lax.rem(z + 3, 4), lax.rem(z + 1, 4)
-    has_above, has_below = s > 0, s < 31
+        wait_all(sc.at[ph, pl.ds(0, 63)], s_sc_r.at[ph])
+        parts = [sc[ph, i] for i in range(4)]
+        for i in range(4, 64):
+            parts[i % 4] += sc[ph, i]
+        total = (parts[0] + parts[1]) + (parts[2] + parts[3])
+        return tuple(jnp.broadcast_to(total[:, i : i + 1], (1, 128)) for i in range(3))
 
     def halo_copies(ph):
         def mk(n, src, dst, to):
@@ -431,12 +472,13 @@
 
     bias_adjoint([term_y, term_d], chan, oh, lhs, acc)
     for t in range(TILES):
-        rs0_send[t, 0:8] = acc_tile(acc, 0, t)
-        rs0_send[t, 8:16] = acc_tile(acc, 1, t)
-    pl.semaphore_wait(barrier, 127)
-    scatter(rs0_send, rs0_recv, 0)
+        rs0_send[place(t), 0:8] = acc_tile(acc, 0, t)
+        rs0_send[place(t), 8:16] = acc_tile(acc, 1, t)
+    pl.semaphore_wait(barrier, greeted)
+    pair_send(rs0_send, pr0, 0)
     to_smem.wait()
-    load_j.wait()
+    loads[7].wait()
+    scatter(rs0_send, pr0, rs0_recv, 0)
     adjoint(y, jac, sm_i, cl, seg)
     halo_send(0)
 
@@ -471,8 +513,9 @@
     ))
     bias_adjoint([term_y], chan, oh, lhs, acc)
     for t in range(TILES):
-        rs_send[0, t] = acc_tile(acc, 0, t)
-    scatter(rs_send.at[0], rs_recv.at[0], 1)
+        rs_send[0, place(t)] = acc_tile(acc, 0, t)
+    pair_send(rs_send.at[0], pr.at[0], 1)
+    scatter(rs_send.at[0], pr.at[0], rs_recv.at[0], 1)
     scalars_b(0)
     adjoint(y, jac, sm_i, cl, seg)
     halo_send(1)
@@ -510,8 +553,9 @@
     ))
     bias_adjoint([term_y], chan, oh, lhs, acc)
     for t in range(TILES):
-        rs_send[1, t] = acc_tile(acc, 0, t)
-    scatter(rs_send.at[1], rs_recv.at[1], 2)
+        rs_send[1, place(t)] = acc_tile(acc, 0, t)
+    pair_send(rs_send.at[1], pr.at[1], 2)
+    scatter(rs_send.at[1], pr.at[1], rs_recv.at[1], 2)
     scalars_b(1)
     adjoint(y, jac, sm_i, cl, seg)
     halo_send(2)
@@ -525,10 +569,10 @@
         return 0
 
     lax.fori_loop(2, 34, solved, 0)
-    store_x = pltpu.make_async_copy(xs, out_x, s_load.at[2])
+    store_x = pltpu.make_async_copy(xs, out_x, s_load.at[9])
     store_x.start()
     for t in range(10):
-        at = z * 10 + t
+        at = (t % 2) * 20 + z * 5 + t // 2
         out_b[:, t * 128 : (t + 1) * 128] = mix * zt[0, at] + alpha1 * zt[1, at]
 
     @pl.when(owner)
@@ -547,13 +591,14 @@
     scalars_a(2, (rr_state + sum8(ob[7] * ob[7]),))
     scalars_b(2)
     rr2, _, _ = scalars_c(2)
-    lane = lax.broadcasted_iota(i32, (1, 128), 1)
     out_n[...] = jnp.sqrt(jnp.where(lane == 0, rr0, jnp.where(lane == 1, rr1, rr2)))
 
-    for ph, ref in ((0, rs0_send), (1, rs_send.at[0]), (2, rs_send.at[1])):
+    for ph, ref in ((0, pr0), (1, pr.at[0]), (2, pr.at[1])):
+        wait_all(ref, s_pr_s.at[ph])
+
         @pl.when(owner)
         def _(ph=ph, ref=ref):
-            wait_all(ref.at[pl.ds(0, TILES - 1)], s_rs_s.at[ph])
+            wait_all(ref.at[pl.ds(0, 19)], s_rs_s.at[ph])
 
         @pl.when(jnp.logical_not(owner))
         def _(ph=ph, ref=ref):
@@ -562,18 +607,46 @@
     @pl.when(owner)
     def _():
         for k in range(2):
-            wait_all(rs_recv.at[0, pl.ds(0, 127)], s_ag_s.at[k])
-
+            wait_all(rs_recv.at[0, pl.ds(0, 63)], s_ag_s.at[k])
+
+    for k in range(2):
+        relay(k).wait_send()
     for ph in range(3):
         halo_done(ph)
-        wait_all(sca.at[ph, pl.ds(0, 7)], s_sc_s.at[ph, 0])
-        wait_all(scb.at[ph, pl.ds(0, 15)], s_sc_s.at[ph, 1])
+        scalar_pair(ph).wait_send()
+        wait_all(sc.at[ph, pl.ds(0, 63)], s_sc_s.at[ph])
     store_x.wait()
+
+
+def finish(x_in, b_in, n_in, x_out, b_out, n_out, hold, held_b, sem):
+    first = pltpu.make_async_copy(b_in, held_b, sem.at[0])
+    first.start()
+    rows = LAT // PIECES
+    come = []
+    for i in range(PIECES):
+        part = pl.ds(i * rows, rows)
+        cp = pltpu.make_async_copy(x_in.at[part], hold.at[part], sem.at[2 + i])
+        cp.start()
+        come.append(cp)
+    n_out[...] = n_in[:, 0:3]
+    first.wait()
+    second = pltpu.make_async_copy(held_b, b_out, sem.at[1])
+    second.start()
+    go = [second]
+    for i, cp in enumerate(come):
+        part = pl.ds(i * rows, rows)
+        cp.wait()
+        out = pltpu.make_async_copy(hold.at[part], x_out.at[part], sem.at[2 + PIECES + i])
+        out.start()
+        go.append(out)
+    for cp in go:
+        cp.wait()
 
 
 def body(innovations, obs_precision, jacobian, predictors, obs_column, obs_channel, obs_count, smoothing, bias_precision):
     vm = pl.BlockSpec(memory_space=pltpu.VMEM)
     hbm = pl.BlockSpec(memory_space=pl.ANY)
+    src = pl.BlockSpec(memory_space=pltpu.HBM)
     sq = (LINES, 128)
     V = pltpu.VMEM
     D = pltpu.SemaphoreType.DMA
@@ -585,18 +658,21 @@
             jax.ShapeDtypeStruct((NPRED, 1280), f32),
             jax.ShapeDtypeStruct((1, 128), f32),
         ),
-        in_specs=[vm, vm, hbm, vm, vm, vm, pl.BlockSpec(memory_space=pltpu.SMEM), vm, vm],
+        in_specs=[src] * 6 + [pl.BlockSpec(memory_space=pltpu.SMEM), src, src],
         out_specs=(hbm, vm, vm),
         scratch_shapes=[
+            V(sq, f32), V(sq, f32), V((NPRED, 16384), f32), V(sq, i32), V(sq, i32), V((1, LEV), f32), V((NPRED, 1280), f32),
             V((LINES, 128, LEV), bf16), V((LINES, 256, 128), bf16), V((KL, 640, 128), bf16), V((640, 256), f32), V((320, 256), bf16),
             V(sq, f32), V(sq, f32), V(sq, f32), V(sq, f32),
             V((LAT, 2 * LON, LEV), bf16), V((LINES, LON, LEV), f32),
             V((3, 36, 80, LEV), f32), V((36, 80, LEV), f32), V((36, 80, LEV), f32), V((36, 80, LEV), f32),
             V((LAT, LON, LEV), f32), V((3, 2, 64, LEV), f32), V((3, 2, 64, LEV), f32), V((3, 4, 8, LEV), f32),
-            V((TILES, 16, 128), f32), V((128, 16, 128), f32), V((2, TILES, 8, 128), f32), V((2, 128, 8, 128), f32),
-            V((2, TILES, 8, 128), f32), V((3, 8, 8, 128), f32), V((3, 16, 8, 128), f32), V((8, 8, 128), f32),
+            V((TILES, 16, 128), f32), V((20, 16, 128), f32), V((64, 16, 128), f32),
+            V((2, TILES, 8, 128), f32), V((2, 20, 8, 128), f32), V((2, 64, 8, 128), f32),
+            V((2, TILES, 8, 128), f32), V((3, 2, 1, 128), f32), V((3, 64, 1, 128), f32), V((8, 8, 128), f32),
             V((8, 128), i32), V(sq, i32), pltpu.SMEM((8, 128), i32),
-            D((3,)), D((3, 8)), D((3, 8)), D((3,)), D((3,)), D((2,)), D((2,)), D((3, 2)), D((3, 2)),
+            D((10,)), D((3, 8)), D((3, 8)), D((3,)), D((3,)), D((3,)), D((3,)), D((2,)), D((2,)), D((2,)), D((2,)),
+            D((3,)), D((3,)), D((3,)), D((3,)),
         ],
         compiler_params=pltpu.CompilerParams(
             collective_id=0, has_side_effects=True, vmem_limit_bytes=62 * 2**20
@@ -605,7 +681,20 @@
         innovations.reshape(sq), obs_precision.reshape(sq), jacobian.reshape(LINES, 128, LEV), predictors,
         obs_column.reshape(sq), obs_channel.reshape(sq), obs_count, smoothing.reshape(1, LEV), bias_precision,
     )
-    return out[0], out[1], out[2][0, :3]
+    done = pl.pallas_call(
+        finish,
+        name="finish",
+        out_shape=(
+            jax.ShapeDtypeStruct((LAT, LON, LEV), f32),
+            jax.ShapeDtypeStruct((NPRED, 1280), f32),
+            jax.ShapeDtypeStruct((1, 3), f32),
+        ),
+        in_specs=[hbm, hbm, vm],
+        out_specs=(hbm, hbm, vm),
+        scratch_shapes=[V((LAT, LON, LEV), f32), V((NPRED, 1280), f32), D((2 + 2 * PIECES,))],
+        compiler_params=pltpu.CompilerParams(vmem_limit_bytes=62 * 2**20),
+    )(*out)
+    return done[0], done[1], done[2][0]
 
 
 def solution(mesh):

time: 90.5 us -> 85 us (0.939)
  local copies, waits for them, and re-layouts: 4.79 us -> 0 us
    unnamed x2 -> x0, local copies, waits for them, and re-layouts: 3.7 us -> none
    pallas_call x1, Pallas kernels: 84 us -> 80.4 us  [body(): pl.pallas_call(kernel, name='pcg', out_shape=(jax.ShapeDtypeStruct((LAT,...]
    pallas_call x0 -> x1, Pallas kernels: none -> 3.2 us  [body(): pl.pallas_call(finish, name='finish', out_shape=(jax.ShapeDtypeStruct((LA...]
    squeeze x1 -> x0, local copies, waits for them, and re-layouts: 1.09 us -> none  [body(): return (out[0], out[1], out[2][0, :3])]
where the time goes in v2:
time: 85 us; the launch traced here: 84.9 us
  Pallas kernels  83.6 us (98%)
  between operations  1.29 us (2%)
    pallas_call x1, Pallas kernels, body(): pl.pallas_call(kernel, name='pcg', out_shape=(jax.ShapeDtypeStruct((LAT,...  80.4 us
    pallas_call x1, Pallas kernels, body(): pl.pallas_call(finish, name='finish', out_shape=(jax.ShapeDtypeStruct((LA...  3.2 us

profile of v2, /device:TPU:0, one launch (start us, length us, event | category | flops | bytes accessed | tf_op | source)
XLA Modules:
  0.0 84.9 jit_solution(16996565323898417183)
XLA Ops:
  1.3 80.4 %pcg.1 = (f32[32,64,128]{2,1,0:T(8,128)}, f32[8,1280]{1,0:T(8,128)}, f32[1,128]{1,0:T(1,128)}) custom-call(f32[128,128]{1,0:T(8,128)} %bitcast.8, f32[128,128]{1,0:T(8,128)} %bitcast.9, bf16[128,128,128]{2,1,0:T(8,128)(2,1)} %bitcast.7, f32[8,16384]{1,0:T(8,128)} %pred_hbm.1, s32[128,128]{1,0:T(8,128)} %bitcast.10, s32[128,128]{1,0:T(8,128)} %bitcast.11, ...), custom_call_target="tpu_custom_call" | custom-call | tf_op jit(solution)/shard_map/pcg/pallas_call | solution.py:653
  81.7 3.2 %finish.1 = (f32[32,64,128]{2,1,0:T(8,128)}, f32[8,1280]{1,0:T(8,128)}, f32[1,3]{1,0:T(1,128)}) custom-call(f32[32,64,128]{2,1,0:T(8,128)} %get-tuple-element.9.x_in, f32[8,1280]{1,0:T(8,128)} %get-tuple-element.10.b_in, f32[1,128]{1,0:T(1,128)} %get-tuple-element.11.n_in), custom_call_target="tpu_custom_call" | custom-call | tf_op jit(solution)/shard_map/finish/pallas_call | solution.py:684

commit v3 on v2

--- a/solution.py
+++ b/solution.py
@@ -112,30 +112,20 @@
     lax.fori_loop(0, LINES // UN, step, jnp.zeros((LON, 128), f32))
 
 
-def make_hot(ch_ref, oh):
-    iota = lax.broadcasted_iota(i32, (256, 128), 0).astype(f32).astype(bf16)
-    one, zero = jnp.ones((), bf16), jnp.zeros((), bf16)
-
-    def step(i, _):
-        for u in range(8):
-            b = i * 8 + u
-            ch = bc((ch_ref[pl.ds(b, 1), :] & 255).astype(f32), 16).astype(bf16)
-            for j in range(0, 256, 16):
-                oh[b, j : j + 16] = jnp.where(iota[j : j + 16] == ch, one, zero)
-        return 0
-
-    lax.fori_loop(0, LINES // 8, step, 0)
-
-
-def bias_adjoint(terms, ch_ref, oh, lhs, acc):
+def bias_adjoint(terms, ch_ref, oh, lhs, acc, fill=False):
     n = len(terms)
     rows, kl = 320 * n, KL // n
-    zero = jnp.zeros((), bf16)
+    one, zero = jnp.ones((), bf16), jnp.zeros((), bf16)
+    iota = lax.broadcasted_iota(i32, (256, 128), 0).astype(f32).astype(bf16)
 
     def step(c, _):
         for l in range(kl):
             b = c * kl + l
             hb = bc((ch_ref[pl.ds(b, 1), :] >> 8).astype(f32), 16).astype(bf16)
+            if fill:
+                ch = bc((ch_ref[pl.ds(b, 1), :] & 255).astype(f32), 16).astype(bf16)
+                for j in range(0, 256, 16):
+                    oh[b, j : j + 16] = jnp.where(iota[j : j + 16] == ch, one, zero)
             sts = [jnp.concatenate(split(f(b)), axis=0) for f in terms]
             for h in range(20):
                 m = hb == jnp.asarray(h, bf16)
@@ -194,7 +184,10 @@
             gp[ph, r] = jnp.zeros((80, 128), f32)
 
     def chips(f):
-        for d in range(1, 64):
+        def hops(d):
+            return sum(min(v, 4 - v) for v in (d // 16, d // 4 % 4, d % 4))
+
+        for d in sorted(range(1, 64), key=hops, reverse=True):
             f((xs4[d // 16], ys4[d // 4 % 4], c, zs4[d % 4]))
 
     above, below = coords(s - 1), coords(s + 1)
@@ -240,7 +233,6 @@
     iv[5:8] = jnp.zeros((3, 128), i32)
     to_smem = pltpu.make_async_copy(iv, sm_i, s_load.at[8])
     to_smem.start()
-    make_hot(chan, oh)
     cl[...] = col[...] & 63
 
     for i in range(8):
@@ -470,7 +462,7 @@
         p = pred[:, lanes(b)]
         return p * p * w[pl.ds(b, 1), :]
 
-    bias_adjoint([term_y, term_d], chan, oh, lhs, acc)
+    bias_adjoint([term_y, term_d], chan, oh, lhs, acc, fill=True)
     for t in range(TILES):
         rs0_send[place(t), 0:8] = acc_tile(acc, 0, t)
         rs0_send[place(t), 8:16] = acc_tile(acc, 1, t)

time: 85 us -> 83.4 us (0.981)
  Pallas kernels: 83.6 us -> 81.9 us
    pallas_call x1, Pallas kernels: 80.4 us -> 78.7 us  [body(): pl.pallas_call(kernel, name='pcg', out_shape=(jax.ShapeDtypeStruct((LAT,...]
where the time goes in v3:
time: 83.4 us; the launch traced here: 83.2 us
  Pallas kernels  81.9 us (98%)
  between operations  1.29 us (2%)
    pallas_call x1, Pallas kernels, body(): pl.pallas_call(kernel, name='pcg', out_shape=(jax.ShapeDtypeStruct((LAT,...  78.7 us
    pallas_call x1, Pallas kernels, body(): pl.pallas_call(finish, name='finish', out_shape=(jax.ShapeDtypeStruct((LA...  3.2 us

profile of v3, /device:TPU:0, one launch (start us, length us, event | category | flops | bytes accessed | tf_op | source)
XLA Modules:
  0.0 83.2 jit_solution(705122849307532317)
XLA Ops:
  1.3 78.7 %pcg.1 = (f32[32,64,128]{2,1,0:T(8,128)}, f32[8,1280]{1,0:T(8,128)}, f32[1,128]{1,0:T(1,128)}) custom-call(f32[128,128]{1,0:T(8,128)} %bitcast.8, f32[128,128]{1,0:T(8,128)} %bitcast.9, bf16[128,128,128]{2,1,0:T(8,128)(2,1)} %bitcast.7, f32[8,16384]{1,0:T(8,128)} %pred_hbm.1, s32[128,128]{1,0:T(8,128)} %bitcast.10, s32[128,128]{1,0:T(8,128)} %bitcast.11, ...), custom_call_target="tpu_custom_call" | custom-call | tf_op jit(solution)/shard_map/pcg/pallas_call | solution.py:645
  80.0 3.2 %finish.1 = (f32[32,64,128]{2,1,0:T(8,128)}, f32[8,1280]{1,0:T(8,128)}, f32[1,3]{1,0:T(1,128)}) custom-call(f32[32,64,128]{2,1,0:T(8,128)} %get-tuple-element.9.x_in, f32[8,1280]{1,0:T(8,128)} %get-tuple-element.10.b_in, f32[1,128]{1,0:T(1,128)} %get-tuple-element.11.n_in), custom_call_target="tpu_custom_call" | custom-call | tf_op jit(solution)/shard_map/finish/pallas_call | solution.py:676
